TPU v7x, 16 devices: a whole 2x2x2 slice. The times are simulated.
16 devices in a mesh: data: 4 (over z, y), expert: 4 (over x, core).
Axes of the slice: x: 2, y: 2, z: 2, core: 2. Of those that a mesh axis runs over, the one named last changes fastest.
Arguments:
- x_tok: bfloat16 [512, 2048], P(('data', 'expert')), parts along dimension 0
- topk_idx: int32 [512, 8], P(('data', 'expert')), parts along dimension 0
- topk_w: float32 [512, 8], P(('data', 'expert')), parts along dimension 0
- w_up: bfloat16 [64, 2048, 1024], P('expert')
- w_down: bfloat16 [64, 1024, 2048], P('expert')
Outputs:
- output: bfloat16 [512, 2048], P(('data', 'expert')), parts along dimension 0
There are 4 independent parts. A program takes and returns all parts, laid end to end along the dimension named above; an argument that names none is the same for every part.
All inputs are finite; a program needn't handle non-finite values.
Results may differ from a plain program's by a relative error of at most 0.00126.
Values are sent between devices in bfloat16 or wider.
A program may use at most 1 GiB of HBM per device.

v0:
```python
import jax
import jax.numpy as jnp
from jax import lax
from jax.sharding import PartitionSpec as P, NamedSharding


def route_slots(idx_loc, n_exp, slot_cap):
    top_k = idx_loc.shape[1]
    pair_exp = idx_loc.reshape(-1)
    n_pairs = pair_exp.shape[0]
    sort_order = jnp.argsort(pair_exp, stable=True)
    pair_rank = jnp.argsort(sort_order, stable=True)
    counts = jnp.bincount(pair_exp, length=n_exp)
    starts = jnp.cumsum(counts) - counts
    slot_src = jnp.minimum(starts[:, None] + jnp.arange(slot_cap)[None, :], n_pairs - 1)
    slot_tok = (sort_order[slot_src] // top_k).reshape(-1)
    pair_slot = pair_exp * slot_cap + pair_rank - starts[pair_exp]
    return slot_tok, pair_slot


def solution(mesh):
    group_size = mesh.shape['expert']

    def local_moe(x_loc, idx_loc, gate_loc, up_loc, down_loc):
        tok_dev, d_model = x_loc.shape
        top_k = idx_loc.shape[1]
        exp_local = up_loc.shape[0]
        n_exp = exp_local * group_size
        slot_cap = min(4, n_exp // top_k) * tok_dev * top_k // n_exp
        slot_tok, pair_slot = route_slots(idx_loc, n_exp, slot_cap)
        send_rows = jnp.take(x_loc, slot_tok, axis=0).reshape(group_size, exp_local, slot_cap, d_model)
        recv_rows = lax.all_to_all(send_rows, 'expert', 0, 0, tiled=True)
        hidden = jnp.einsum('secm,emf->secf', recv_rows, up_loc, preferred_element_type=jnp.float32)
        hidden = jax.nn.gelu(hidden, approximate=True).astype(jnp.bfloat16)
        expert_out = jnp.einsum('secf,efm->secm', hidden, down_loc, preferred_element_type=jnp.float32).astype(jnp.bfloat16)
        back_rows = lax.all_to_all(expert_out, 'expert', 0, 0, tiled=True).reshape(n_exp * slot_cap, d_model)
        pair_out = jnp.take(back_rows, pair_slot, axis=0).reshape(tok_dev, top_k, d_model)
        combined = jnp.sum(gate_loc[:, :, None] * pair_out.astype(jnp.float32), axis=1)
        return combined.astype(jnp.bfloat16)

    tok_spec = P(('data', 'expert'), None)
    w_spec = P('expert', None, None)
    return jax.shard_map(local_moe, mesh=mesh, in_specs=(tok_spec, tok_spec, tok_spec, w_spec, w_spec), out_specs=tok_spec, check_vma=False)
```

profile of v0, /device:TPU:0, one launch (start us, length us, event | category | flops | bytes accessed | tf_op | source)
XLA Modules:
  0.0 186.2 jit_solution(16297268326736042309)
XLA Ops:
  0.0 0.8 copy.16
  0.8 0.1 reshape.223
  0.9 0.1 reshape.222
  1.0 2.3 %scatter_custom_fusion = s32[64]{0:T(128)S(1)} fusion(s32[256]{0:T(256)S(1)} %bitcast.36, s32[256]{0:T(256)S(1)} %broadcast.197, s32[]{:T(128)} %constant.33.clone.1), kind=kCustom, calls=%fused_computation.46 | custom fusion | flops 256 | bytes 260 | tf_op jit(solution)/shard_map/scatter-add | solution.py:13
  3.3 0.1 copy.18
  3.4 0.1 reduce-window.9
  3.5 0.1 reduce
  3.6 0.1 compare_select_fusion.1
  3.8 3.2 %sort.31 = (s32[256]{0:T(256)}, s32[256]{0:T(256)S(1)}) sort(s32[256]{0:T(256)S(1)} %reshape.222, s32[256]{0:T(256)S(1)} %iota.13), dimensions={0}, to_apply=%region_0.0 | sort | flops 2048 | bytes 4096 | tf_op jit(solution)/shard_map/jit(argsort)/sort | solution.py:11
  7.0 6.9 %gather_fusion.1 = s32[1024]{0:T(1024)S(1)} fusion(s32[256]{0:T(256)S(1)} %get-tuple-element.7, s32[1024]{0:T(1024)S(1)} %broadcast_clamp_fusion.1), kind=kCustom, calls=%fused_computation.1 | custom fusion | bytes 12288 | tf_op jit(solution)/shard_map/gather | solution.py:16
  14.0 6.0 %gather_fusion.2 = bf16[1024,2048]{1,0:T(8,128)(2,1)} fusion(bf16[32,2048]{1,0:T(8,128)(2,1)S(1)} %copy-done, s32[1024]{0:T(1024)S(1)} %broadcast_clamp_fusion), kind=kCustom, calls=%fused_computation.2 | custom fusion | bytes 8392704 | tf_op jit(solution)/shard_map/jit(_take)/gather | solution.py:31
  20.0 2.6 %broadcast_select_fusion = bf16[4,16,16,2048]{3,2,1,0:T(8,128)(2,1)S(1)} fusion(bf16[4,16,16,2048]{3,2,1,0:T(8,128)(2,1)} %bitcast.32, pred[4,16,16]{2,1,0:T(8,128)(4,1)S(1)} %compare_and_fusion), kind=kLoop, calls=%fused_computation.20 | loop fusion | flops 2097152 | bytes 8389632 | tf_op jit(solution)/shard_map/jit(_take)/select_n | solution.py:31
  22.7 52.4 %all_to_all.10 = bf16[4,16,16,2048]{3,2,1,0:T(8,128)(2,1)} all-to-all(bf16[4,16,16,2048]{3,2,1,0:T(8,128)(2,1)S(1)} %broadcast_select_fusion), channel_id=1, replica_groups=mesh['data'=4,'expert'=4] {'expert'}, dimensions={0} | all-to-all | bytes 8388608 | tf_op jit(solution)/shard_map/all_to_all | solution.py:32
  75.1 24.7 %fusion.11 = bf16[4,16,16,1024]{3,2,0,1:T(8,128)(2,1)S(1)} fusion(bf16[16,2048,1024]{2,1,0:T(8,128)(2,1)} %param.8, bf16[4,16,16,2048]{3,2,1,0:T(8,128)(2,1)} %all_to_all.10), kind=kOutput, calls=%fused_computation.17 | convolution fusion | flops 4304404480 | bytes 73400320 | tf_op jit(solution)/shard_map/secm,emf->secf/dot_general | solution.py:33
  99.8 23.7 %convert_bitcast_fusion = bf16[4,16,16,2048]{3,2,0,1:T(8,128)(2,1)S(1)} fusion(bf16[4,16,16,1024]{3,2,0,1:T(8,128)(2,1)S(1)} %fusion.11, bf16[16,1024,2048]{2,1,0:T(8,128)(2,1)} %param.9), kind=kOutput, calls=%fused_computation.19 | convolution fusion | flops 4297064448 | bytes 73400320 | tf_op jit(solution)/shard_map/secf,efm->secm/dot_general | solution.py:35
  123.5 2.5 %copy.20 = bf16[4,16,16,2048]{3,2,1,0:T(8,128)(2,1)} copy(bf16[4,16,16,2048]{3,2,0,1:T(8,128)(2,1)S(1)} %convert_bitcast_fusion) | data formatting | bytes 8388608 | tf_op jit(solution)/shard_map/convert_element_type | solution.py:35
  126.0 5.2 %all-to-all-start.1 = ((bf16[4,16,16,2048]{3,2,1,0:T(8,128)(2,1)}), bf16[4,16,16,2048]{3,2,1,0:T(8,128)(2,1)}, u32[]{:S(2)}, u32[]{:S(2)}) async-start(bf16[4,16,16,2048]{3,2,1,0:T(8,128)(2,1)} %copy.20), calls=%async_computation.1 | async-start | bytes 8388608 | tf_op jit(solution)/shard_map/all_to_all | solution.py:36
  131.2 1.9 %gather_fusion = s32[256]{0:T(256)S(1)} fusion(s32[64]{0:T(128)S(1)} %sub.14, s32[1024]{0:T(1024)S(1)} %pad_clamp_fusion.1), kind=kCustom, calls=%fused_computation | custom fusion | bytes 3072 | tf_op jit(solution)/shard_map/gather | solution.py:17
  133.1 3.2 %sort.32 = (s32[256]{0:T(256)}, s32[256]{0:T(256)S(1)}) sort(s32[256]{0:T(256)S(1)} %get-tuple-element.7, s32[256]{0:T(256)S(1)} %iota.14), dimensions={0}, to_apply=%region_1.2 | sort | flops 2048 | bytes 4096 | tf_op jit(solution)/shard_map/jit(argsort)/sort | solution.py:12
  136.3 0.1 broadcast_in_dim.38
  136.4 0.1 copy.15
  136.5 42.4 %all-to-all-done.1 = bf16[4,16,16,2048]{3,2,1,0:T(8,128)(2,1)} async-done(((bf16[4,16,16,2048]{3,2,1,0:T(8,128)(2,1)}), bf16[4,16,16,2048]{3,2,1,0:T(8,128)(2,1)}, u32[]{:S(2)}, u32[]{:S(2)}) %all-to-all-start.1) | async-done | bytes 4194336 | tf_op jit(solution)/shard_map/all_to_all | solution.py:36
  178.9 5.1 %gather_fusion.3 = bf16[256,2048]{1,0:T(8,128)(2,1)S(1)} fusion(bf16[1024,2048]{1,0:T(8,128)(2,1)} %bitcast.12, s32[1024]{0:T(1024)S(1)} %pad_clamp_fusion), kind=kCustom, calls=%fused_computation.3 | custom fusion | bytes 2098176 | tf_op jit(solution)/shard_map/jit(_take)/gather | solution.py:37
  184.0 2.2 %multiply_reduce_fusion = bf16[32,2048]{1,0:T(8,128)(2,1)} fusion(bf16[256,2048]{1,0:T(8,128)(2,1)S(1)} %gather_fusion.3, f32[32,8]{1,0:T(8,128)S(1)} %copy.15, pred[32,8]{1,0:T(8,128)(4,1)S(1)} %broadcast_in_dim.38), kind=kLoop, calls=%fused_computation.21 | loop fusion | flops 2031616 | bytes 1180928 | tf_op jit(solution)/shard_map/reduce_sum | solution.py:38
  (18 shorter events, 0.3 us)
Async XLA Ops:
  0.0 14.0 %copy-start = (bf16[32,2048]{1,0:T(8,128)(2,1)S(1)}, bf16[32,2048]{1,0:T(8,128)(2,1)}, u32[]{:S(2)}) copy-start(bf16[32,2048]{1,0:T(8,128)(2,1)} %param.5) | copy-start | bytes 393220
  126.0 10.4 %copy-start.1 = (f32[32,8]{0,1:T(8,128)S(1)}, f32[32,8]{0,1:T(8,128)}, u32[]{:S(2)}) copy-start(f32[32,8]{0,1:T(8,128)} %param.7) | copy-start | bytes 3076
  126.0 52.9 %all-to-all-start.1 = ((bf16[4,16,16,2048]{3,2,1,0:T(8,128)(2,1)}), bf16[4,16,16,2048]{3,2,1,0:T(8,128)(2,1)}, u32[]{:S(2)}, u32[]{:S(2)}) async-start(bf16[4,16,16,2048]{3,2,1,0:T(8,128)(2,1)} %copy.20), calls=%async_computation.1 | async-start | bytes 8388608 | tf_op jit(solution)/shard_map/all_to_all | solution.py:36
where the time goes:
time: 186 us
  blocking collectives  52.4 us (28%)
  matrix products  48.4 us (26%)
  waiting for transfers between devices  42.4 us (23%)
  local copies, waits for them, and re-layouts  23.7 us (13%)
  other arithmetic  13.8 us (7%)
  starting transfers between devices  5.17 us (3%)
    all_to_all x1, blocking collectives, local_moe(): recv_rows = lax.all_to_all(send_rows, 'expert', 0, 0, tiled=True)  52.4 us
    all_to_all x1, waiting for transfers between devices, local_moe(): lax.all_to_all(expert_out, 'expert', 0, 0, tiled=True)  42.4 us
    dot_general x1, matrix products, local_moe(): jnp.einsum('secm,emf->secf', recv_rows, up_loc, preferred_element_type=jn...  24.7 us
    dot_general x1, matrix products, local_moe(): jnp.einsum('secf,efm->secm', hidden, down_loc, preferred_element_type=jnp...  23.7 us
    gather x2, local copies, waits for them, and re-layouts, route_slots(): slot_tok = (sort_order[slot_src] // top_k).reshape(-1)  6.93 us
    gather x1, local copies, waits for them, and re-layouts, local_moe(): jnp.take(x_loc, slot_tok, axis=0)  6.02 us
    all_to_all x1, starting transfers between devices, local_moe(): lax.all_to_all(expert_out, 'expert', 0, 0, tiled=True)  5.17 us
    gather x1, local copies, waits for them, and re-layouts, local_moe(): jnp.take(back_rows, pair_slot, axis=0).reshape(tok_dev, top_k, d_model)  5.09 us
  transfers between devices with their start and end apart: 1, of which 1 were waited for; matrix products, arithmetic and copies ran while one was open for 3% of the time, Pallas kernels for 0%

commit v1 on v0

v1 whole, which is shorter than its diff:
```python
import functools

import jax
import jax.numpy as jnp
from jax import lax
from jax.experimental import pallas as pl
from jax.experimental.pallas import tpu as pltpu
from jax.sharding import PartitionSpec as P

MESH = pl.DeviceIdType.MESH
POOL = 2
RING = 24
SUB = 256
GELU_C = 0.7978845608028654


def gelu(v):
    return v * (0.5 + 0.5 * jnp.tanh(v * (GELU_C + (GELU_C * 0.044715) * (v * v))))


def kernel(pool, x_hbm, idx_hbm, gate_hbm, up_hbm, down_hbm, out_hbm,
           ring, xall, idx_all, gate_all, gb, hbuf, pacc, d2d_in, ssum, ici_in, out_v,
           ring_sem, load_sem, msend, mrecv, d2d_send, d2d_recv, ici_send, ici_recv, out_sem):
    data, expert = lax.axis_index("data"), lax.axis_index("expert")
    core = expert % 2
    y = data % pool
    chip = y * 2 + expert // 2
    me = chip * 2 + core
    chips = 2 * pool
    ranks = 2 * chips
    tok = x_hbm.shape[0]
    top_k = idx_hbm.shape[1]
    rows = ranks * tok
    n_loc = up_hbm.shape[0]
    n_exp = n_loc // pool
    width = ring.shape[3]
    half = ring.shape[2]
    n_up = up_hbm.shape[3] // width
    n_chunk = down_hbm.shape[2] // width
    n_pair = n_exp // 2
    up_items = n_exp * n_up
    items = up_items + n_chunk * n_pair
    first = y * n_exp

    partner = (data, expert + 1 - 2 * core)

    def chip_dev(k):
        ex = expert if k % 2 == 0 else lax.rem(expert + 2, 4)
        da = data if k < 2 else data + 1 - 2 * y
        return (da, ex)

    def up_copy(i):
        e, n = i // n_up, i % n_up
        return pltpu.make_async_copy(
            up_hbm.at[first + e, :, :, pl.ds(pl.multiple_of(n * width, width), width)],
            ring.at[i % RING], ring_sem.at[i % RING])

    def down_copy(i):
        j = i - up_items
        c, p = j // n_pair, j % n_pair
        return pltpu.make_async_copy(
            down_hbm.at[pl.ds(first + 2 * p, 2), :, pl.ds(pl.multiple_of(c * width, width), width)],
            ring.at[i % RING], ring_sem.at[i % RING])

    def fetch(i):
        @pl.when(i < up_items)
        def _():
            up_copy(i).start()

        @pl.when(jnp.logical_and(i >= up_items, i < items))
        def _():
            down_copy(i).start()

    def own(ref):
        return ref.at[pl.ds(pl.multiple_of(me * tok, tok), tok)]

    loads = [pltpu.make_async_copy(src, own(dst), load_sem.at[k])
             for k, (src, dst) in enumerate(((idx_hbm, idx_all), (gate_hbm, gate_all), (x_hbm, xall)))]
    for cp in loads:
        cp.start()
    for i in range(min(RING, items)):
        (up_copy if i < up_items else down_copy)(i).start()

    barrier = pltpu.get_barrier_semaphore()
    for dev in [partner] + [chip_dev(k) for k in range(1, chips)]:
        pl.semaphore_signal(barrier, inc=1, device_id=dev, device_id_type=MESH)
    pl.semaphore_wait(barrier, chips)

    def rank_rows(ref, r):
        return ref.at[pl.ds(pl.multiple_of(r * tok, tok), tok)]

    def send(ref, kind, r, slot, dev):
        return pltpu.make_async_remote_copy(
            src_ref=rank_rows(ref, r), dst_ref=rank_rows(ref, r),
            send_sem=msend.at[kind, slot], recv_sem=mrecv.at[kind, r],
            device_id=dev, device_id_type=MESH)

    bufs = (idx_all, gate_all, xall)
    other = [(chip ^ k) * 2 + core for k in range(chips)]
    started = []
    for kind, ref in enumerate(bufs):
        loads[kind].wait()
        for k in range(1, chips):
            cp = send(ref, kind, me, k - 1, chip_dev(k))
            cp.start()
            started.append(cp)
        cp = send(ref, kind, me, chips - 1, partner)
        cp.start()
        started.append(cp)
    for kind, ref in enumerate(bufs):
        for k in range(1, chips):
            send(ref, kind, other[k], 0, partner).wait_recv()
            cp = send(ref, kind, other[k], chips - 1 + k, partner)
            cp.start()
            started.append(cp)
        if kind == 1:
            for kk in range(2):
                for k in range(chips):
                    send(bufs[kk], kk, (chip ^ k) * 2 + 1 - core, 0, partner).wait_recv()
            for e in range(n_exp):
                eid = expert * n_loc + first + e
                hit = jnp.where(idx_all[...] == eid, gate_all[...], -1.0)
                gb[e] = jnp.broadcast_to(jnp.max(hit, axis=1, keepdims=True), (rows, 128))
    for k in range(chips):
        send(xall, 2, (chip ^ k) * 2 + 1 - core, 0, partner).wait_recv()

    def up_step(i, carry):
        e, n = i // n_up, i % n_up
        slot = i % RING
        up_copy(i).wait()
        keep = gb[e] >= 0.0
        for s in range(width // SUB):
            cols = pl.ds(s * SUB, SUB)
            acc = jnp.dot(xall[:, :half], ring[slot, 0, :, cols], preferred_element_type=jnp.float32)
            acc += jnp.dot(xall[:, half:], ring[slot, 1, :, cols], preferred_element_type=jnp.float32)
            for v in range(SUB // 128):
                part = gelu(acc[:, v * 128:(v + 1) * 128])
                hbuf[e, n, :, pl.ds(s * SUB + v * 128, 128)] = jnp.where(keep, part, 0.0).astype(jnp.bfloat16)
        fetch(i + RING)
        return carry

    lax.fori_loop(0, up_items, up_step, 0)

    def d2d(c):
        return pltpu.make_async_remote_copy(
            src_ref=pacc.at[c, :, 1 - core], dst_ref=d2d_in.at[c],
            send_sem=d2d_send.at[c], recv_sem=d2d_recv.at[c], device_id=partner, device_id_type=MESH)

    def ici(c, k):
        return pltpu.make_async_remote_copy(
            src_ref=ssum.at[c, chip ^ k], dst_ref=ici_in.at[c, k - 1],
            send_sem=ici_send.at[c, k - 1], recv_sem=ici_recv.at[c, k - 1],
            device_id=chip_dev(k), device_id_type=MESH)

    def forward(c):
        d2d(c).wait_recv()
        ssum[c] = pacc[c, :, core] + d2d_in[c]
        for k in range(chips - 1, 0, -1):
            ici(c, k).start()

    for c in range(n_chunk):
        def down_step(p, carry, c=c):
            i = up_items + c * n_pair + p
            slot = i % RING
            down_copy(i).wait()
            for s in range(width // SUB):
                cols = pl.ds(s * SUB, SUB)
                for b in range(2):
                    e = 2 * p + b
                    o = jnp.dot(hbuf[e, 0], ring[slot, b, :width, cols], preferred_element_type=jnp.float32)
                    for n in range(1, n_up):
                        o += jnp.dot(hbuf[e, n], ring[slot, b, n * width:(n + 1) * width, cols],
                                     preferred_element_type=jnp.float32)
                    o = o.astype(jnp.bfloat16).astype(jnp.float32)
                    for v in range(SUB // 128):
                        lane = pl.ds(s * SUB + v * 128, 128)
                        term = (gb[e] * o[:, v * 128:(v + 1) * 128]).reshape(chips, 2, tok, 128)
                        pacc[c, :, :, :, lane] += term
            fetch(i + RING)
            return carry

        pacc[c] = jnp.zeros(pacc.shape[1:], jnp.float32)
        lax.fori_loop(0, n_pair, down_step, 0)
        d2d(c).start()
        if c > 0:
            forward(c - 1)
    forward(n_chunk - 1)

    outs = []
    for c in range(n_chunk):
        total = ssum[c, chip]
        for k in range(1, chips):
            ici(c, k).wait_recv()
            total += ici_in[c, k - 1]
        out_v[c] = total.astype(jnp.bfloat16)
        cp = pltpu.make_async_copy(out_v.at[c], out_hbm.at[:, pl.ds(c * width, width)], out_sem.at[c])
        cp.start()
        outs.append(cp)
    for cp in started:
        cp.wait_send()
    for c in range(n_chunk):
        d2d(c).wait_send()
        for k in range(1, chips):
            ici(c, k).wait_send()
        outs[c].wait()


def solution(mesh):
    pool = POOL

    def local_moe(x_loc, idx_loc, gate_loc, up_loc, down_loc):
        tok, d_model = x_loc.shape
        top_k = idx_loc.shape[1]
        n_loc, _, d_ff = up_loc.shape
        chips, ranks = 2 * pool, 4 * pool
        rows = ranks * tok
        n_exp = n_loc // pool
        width = d_ff // 2
        n_chunk = d_model // width
        n_up = d_ff // width
        up4 = up_loc.reshape(n_loc, 2, d_model // 2, d_ff)
        dma, f32, bf16 = pltpu.SemaphoreType.DMA, jnp.float32, jnp.bfloat16
        hbm = pl.BlockSpec(memory_space=pltpu.HBM)
        return pl.pallas_call(
            functools.partial(kernel, pool),
            out_shape=jax.ShapeDtypeStruct((tok, d_model), bf16),
            in_specs=[hbm] * 5,
            out_specs=hbm,
            scratch_shapes=[
                pltpu.VMEM((RING, 2, d_ff, width), bf16),
                pltpu.VMEM((rows, d_model), bf16),
                pltpu.VMEM((rows, top_k), jnp.int32),
                pltpu.VMEM((rows, top_k), f32),
                pltpu.VMEM((n_exp, rows, 128), f32),
                pltpu.VMEM((n_exp, n_up, rows, width), bf16),
                pltpu.VMEM((n_chunk, chips, 2, tok, width), f32),
                pltpu.VMEM((n_chunk, chips, tok, width), f32),
                pltpu.VMEM((n_chunk, chips, tok, width), f32),
                pltpu.VMEM((n_chunk, chips - 1, tok, width), f32),
                pltpu.VMEM((n_chunk, tok, width), bf16),
                dma((RING,)), dma((3,)),
                dma((3, 2 * chips - 1)), dma((3, ranks)),
                dma((n_chunk,)), dma((n_chunk,)),
                dma((n_chunk, chips - 1)), dma((n_chunk, chips - 1)),
                dma((n_chunk,)),
            ],
            compiler_params=pltpu.CompilerParams(
                collective_id=0, has_side_effects=True, vmem_limit_bytes=67043328),
            name="moe",
        )(x_loc, idx_loc, gate_loc, up4, down_loc)

    tok_spec = P(('data', 'expert'), None)
    w_spec = P('expert', None, None)
    return jax.shard_map(local_moe, mesh=mesh, in_specs=(tok_spec, tok_spec, tok_spec, w_spec, w_spec), out_specs=tok_spec, check_vma=False)
```

time: 186 us -> 64.6 us (0.35)
  Pallas kernels: 0 us -> 60.1 us
  blocking collectives: 52.4 us -> 0 us
  matrix products: 48.4 us -> 0 us
  waiting for transfers between devices: 42.4 us -> 0 us
  local copies, waits for them, and re-layouts: 23.7 us -> 4.29 us
  other arithmetic: 13.8 us -> 0 us
  starting transfers between devices: 5.17 us -> 0 us
    pallas_call x0 -> x1, Pallas kernels: none -> 60.1 us  [local_moe(): pl.pallas_call(functools.partial(kernel, pool), out_shape=jax.ShapeDtypeS...]
    all_to_all x1 -> x0, blocking collectives: 52.4 us -> none  [local_moe(): recv_rows = lax.all_to_all(send_rows, 'expert', 0, 0, tiled=True)]
    dot_general x2 -> x0, matrix products: 48.4 us -> none  [the longest x1 24.7 us: local_moe(): jnp.einsum('secm,emf->secf', recv_rows, up_loc, preferred_element_type=jn...]
    all_to_all x1 -> x0, waiting for transfers between devices: 42.4 us -> none  [local_moe(): lax.all_to_all(expert_out, 'expert', 0, 0, tiled=True)]
    gather x5 -> x0, local copies, waits for them, and re-layouts: 19.9 us -> none  [the longest x2 6.93 us: route_slots(): slot_tok = (sort_order[slot_src] // top_k).reshape(-1)]
    sort x2 -> x0, other arithmetic: 6.33 us -> none  [the longest x1 3.17 us: route_slots(): sort_order = jnp.argsort(pair_exp, stable=True)]
    all_to_all x1 -> x0, starting transfers between devices: 5.17 us -> none  [local_moe(): lax.all_to_all(expert_out, 'expert', 0, 0, tiled=True)]
    unnamed x6 -> x3, local copies, waits for them, and re-layouts: 0.88 us -> 4.29 us
  transfers between devices with their start and end apart: 1 -> 0, of which waited for: 1 -> 0; matrix products, arithmetic and copies ran while one was open for 3% -> 0% of each run, Pallas kernels for 0% -> 0%
where the time goes in v1:
time: 64.6 us; the launch traced here: 64.4 us
  Pallas kernels  60.1 us (93%)
  local copies, waits for them, and re-layouts  4.29 us (7%)
    pallas_call x1, Pallas kernels, local_moe(): pl.pallas_call(functools.partial(kernel, pool), out_shape=jax.ShapeDtypeS...  60.1 us
    unnamed x3, local copies, waits for them, and re-layouts  4.29 us

profile of v1, /device:TPU:0, one launch (start us, length us, event | category | flops | bytes accessed | tf_op | source)
XLA Modules:
  0.0 64.4 jit_solution(6507781595598451657)
XLA Ops:
  0.0 1.4 %copy.6.idx_hbm = s32[32,8]{1,0:T(8,128)} copy(s32[32,8]{0,1:T(8,128)} %param.6) | data formatting | bytes 2048 | tf_op args[1]
  1.4 1.4 %copy.7.gate_hbm = f32[32,8]{1,0:T(8,128)} copy(f32[32,8]{0,1:T(8,128)} %param.7) | data formatting | bytes 2048 | tf_op args[2]
  2.7 60.1 %moe.1 = bf16[32,2048]{1,0:T(8,128)(2,1)} custom-call(bf16[32,2048]{1,0:T(8,128)(2,1)} %x_hbm.1, s32[32,8]{1,0:T(8,128)} %copy.6.idx_hbm, f32[32,8]{1,0:T(8,128)} %copy.7.gate_hbm, bf16[16,2,1024,1024]{3,2,1,0:T(8,128)(2,1)} %bitcast.up_hbm, bf16[16,1024,2048]{2,1,0:T(8,128)(2,1)} %down_hbm.1), custom_call_target="tpu_custom_call" | custom-call | tf_op jit(solution)/shard_map/moe/pallas_call | solution.py:224
  62.8 1.6 %copy.9 = bf16[32,2048]{1,0:T(8,128)(2,1)} copy(bf16[32,2048]{1,0:T(8,128)(2,1)} %moe.1) | data formatting | bytes 262144

commit v2 on v1

v2 whole, which is shorter than its diff:
```python
import functools

import jax
import jax.numpy as jnp
from jax import lax
from jax.experimental import pallas as pl
from jax.experimental.pallas import tpu as pltpu
from jax.sharding import PartitionSpec as P

MESH = pl.DeviceIdType.MESH
POOL = 2
RING = 22
SUB = 256
GELU_C = 0.7978845608028654


def gelu(v):
    return v * (0.5 + 0.5 * jnp.tanh(v * (GELU_C + (GELU_C * 0.044715) * (v * v))))


def kernel(pool, cap, x_hbm, idx_hbm, gate_hbm, up_hbm, down_hbm, out_hbm,
           ring, xall, idx_all, gate_all, pmat, cmat, xg, hbuf, obuf, pacc, d2d_in, ssum, ici_in, out_v,
           ring_sem, load_sem, msend, mrecv, d2d_send, d2d_recv, ici_send, ici_recv, out_sem):
    data, expert = lax.axis_index("data"), lax.axis_index("expert")
    core = expert % 2
    y = data % pool
    chips = 2 * pool
    ranks = 2 * chips
    tok = x_hbm.shape[0]
    top_k = idx_hbm.shape[0]
    n_loc = up_hbm.shape[0]
    n_exp = n_loc // pool
    width = ring.shape[3]
    half = ring.shape[2]
    n_up = up_hbm.shape[3] // width
    n_chunk = down_hbm.shape[2] // width
    n_pair = n_exp // 2
    up_items = n_exp * n_up
    items = up_items + n_chunk * n_pair
    first = y * n_exp
    slots = n_exp * cap

    partner = (data, expert + 1 - 2 * core)

    def chip_dev(k):
        ex = expert if k % 2 == 0 else lax.rem(expert + 2, 4)
        da = data if k < 2 else data + 1 - 2 * y
        return (da, ex)

    def up_copy(i):
        e, n = i // n_up, i % n_up
        return pltpu.make_async_copy(
            up_hbm.at[first + e, :, :, pl.ds(pl.multiple_of(n * width, width), width)],
            ring.at[i % RING], ring_sem.at[i % RING])

    def down_copy(i):
        j = i - up_items
        c, p = j // n_pair, j % n_pair
        return pltpu.make_async_copy(
            down_hbm.at[pl.ds(first + 2 * p, 2), :, pl.ds(pl.multiple_of(c * width, width), width)],
            ring.at[i % RING], ring_sem.at[i % RING])

    def fetch(i):
        @pl.when(i < up_items)
        def _():
            up_copy(i).start(priority=1)

        @pl.when(jnp.logical_and(i >= up_items, i < items))
        def _():
            down_copy(i).start(priority=1)

    bufs = (idx_all, gate_all, xall)
    loads = [pltpu.make_async_copy(src, dst.at[0], load_sem.at[k])
             for k, (src, dst) in enumerate(zip((idx_hbm, gate_hbm, x_hbm), bufs))]
    for cp in loads:
        cp.start()
    for i in range(min(RING, items)):
        (up_copy if i < up_items else down_copy)(i).start(priority=1)

    barrier = pltpu.get_barrier_semaphore()
    for dev in [partner] + [chip_dev(k) for k in range(1, chips)]:
        pl.semaphore_signal(barrier, inc=1, device_id=dev, device_id_type=MESH)
    pl.semaphore_wait(barrier, chips)

    started = []

    def send(kind, src, dst, dev):
        cp = pltpu.make_async_remote_copy(
            src_ref=bufs[kind].at[src], dst_ref=bufs[kind].at[dst],
            send_sem=msend.at[kind, dst - 1], recv_sem=mrecv.at[kind, dst],
            device_id=dev, device_id_type=MESH)
        cp.start()
        started.append(cp)

    def arrived(kind, src):
        pltpu.make_async_remote_copy(
            src_ref=bufs[kind].at[src], dst_ref=bufs[kind].at[src],
            send_sem=msend.at[kind, 0], recv_sem=mrecv.at[kind, src],
            device_id=partner, device_id_type=MESH).wait_recv()

    for kind in range(3):
        loads[kind].wait()
        for k in range(chips - 1, 0, -1):
            send(kind, 0, 2 * k, chip_dev(k))
        send(kind, 0, 1, partner)
    for kind in range(2):
        for k in range(1, chips):
            arrived(kind, 2 * k)
            send(kind, 2 * k, 2 * k + 1, partner)
    for kind in range(2):
        for k in range(chips):
            arrived(kind, 2 * k + 1)

    row = lax.broadcasted_iota(jnp.int32, (slots, tok), 0)
    eid = row // cap + (expert * n_loc + first)
    pos = (row % cap).astype(jnp.float32)
    before = (lax.broadcasted_iota(jnp.int32, (tok, tok), 0)
              < lax.broadcasted_iota(jnp.int32, (tok, tok), 1)).astype(jnp.bfloat16)
    for r in range(ranks):
        chose = jnp.zeros((slots, tok), jnp.float32)
        gate = jnp.zeros((slots, tok), jnp.float32)
        for j in range(top_k):
            hit = idx_all[r, j:j + 1, :] == eid
            chose = jnp.where(hit, 1.0, chose)
            gate = jnp.where(hit, gate_all[r, j:j + 1, :], gate)
        seen = jnp.dot(chose.astype(jnp.bfloat16), before, preferred_element_type=jnp.float32)
        one = jnp.logical_and(chose > 0.0, seen == pos)
        pmat[r] = jnp.where(one, 1.0, 0.0).astype(jnp.bfloat16)
        comb = jnp.where(one, gate, 0.0).T
        hi = comb.astype(jnp.bfloat16)
        rest = comb - hi.astype(jnp.float32)
        mid = rest.astype(jnp.bfloat16)
        low = (rest - mid.astype(jnp.float32)).astype(jnp.bfloat16)
        cmat[r, 0:tok] = hi
        cmat[r, tok:2 * tok] = mid
        cmat[r, 2 * tok:] = low

    def gather(r):
        for s in range(xall.shape[2] // SUB):
            cols = slice(s * SUB, (s + 1) * SUB)
            rows = jnp.dot(pmat[r], xall[r, :, cols], preferred_element_type=jnp.float32)
            xg[:, r * cap:(r + 1) * cap, cols] = rows.astype(jnp.bfloat16).reshape(n_exp, cap, SUB)

    gather(0)
    arrived(2, 1)
    gather(1)
    for k in range(1, chips):
        arrived(2, 2 * k)
        send(2, 2 * k, 2 * k + 1, partner)
        gather(2 * k)
    for k in range(1, chips):
        arrived(2, 2 * k + 1)
        gather(2 * k + 1)

    def up_step(e, carry):
        for n in range(n_up):
            i = e * n_up + n
            slot = i % RING
            up_copy(i).wait()
            for s in range(width // SUB):
                cols = slice(s * SUB, (s + 1) * SUB)
                acc = jnp.dot(xg[e, :, :half], ring[slot, 0, :, cols], preferred_element_type=jnp.float32)
                acc += jnp.dot(xg[e, :, half:], ring[slot, 1, :, cols], preferred_element_type=jnp.float32)
                hbuf[e, n, :, cols] = gelu(acc).astype(jnp.bfloat16)
            fetch(i + RING)
        return carry

    lax.fori_loop(0, n_exp, up_step, 0)

    def d2d(c):
        return pltpu.make_async_remote_copy(
            src_ref=pacc.at[c, 1], dst_ref=d2d_in.at[c],
            send_sem=d2d_send.at[c], recv_sem=d2d_recv.at[c], device_id=partner, device_id_type=MESH)

    def ici(c, k):
        return pltpu.make_async_remote_copy(
            src_ref=ssum.at[c, k], dst_ref=ici_in.at[c, k - 1],
            send_sem=ici_send.at[c, k - 1], recv_sem=ici_recv.at[c, k - 1],
            device_id=chip_dev(k), device_id_type=MESH)

    def forward(c):
        d2d(c).wait_recv()
        ssum[c] = pacc[c, 0] + d2d_in[c]
        for k in range(chips - 1, 0, -1):
            ici(c, k).start()

    for c in range(n_chunk):
        for p in range(n_pair):
            i = up_items + c * n_pair + p
            slot = i % RING
            down_copy(i).wait()
            for s in range(width // SUB):
                cols = slice(s * SUB, (s + 1) * SUB)
                for b in range(2):
                    e = 2 * p + b
                    o = jnp.dot(hbuf[e, 0], ring[slot, b, :width, cols], preferred_element_type=jnp.float32)
                    for n in range(1, n_up):
                        o += jnp.dot(hbuf[e, n], ring[slot, b, n * width:(n + 1) * width, cols],
                                     preferred_element_type=jnp.float32)
                    obuf[e, :, cols] = o.astype(jnp.bfloat16)
            if i + RING < items:
                fetch(i + RING)
        for s in range(width // SUB):
            cols = slice(s * SUB, (s + 1) * SUB)
            for r in range(ranks):
                o = obuf[:, r * cap:(r + 1) * cap, cols].reshape(slots, SUB)
                t = jnp.dot(cmat[r], o, preferred_element_type=jnp.float32)
                pacc[c, r % 2, r // 2, :, cols] = t[:tok] + t[tok:2 * tok] + t[2 * tok:]
        d2d(c).start()
        if c > 0:
            forward(c - 1)
    forward(n_chunk - 1)

    outs = []
    for c in range(n_chunk):
        total = ssum[c, 0]
        for k in range(1, chips):
            ici(c, k).wait_recv()
            total += ici_in[c, k - 1]
        out_v[c] = total.astype(jnp.bfloat16)
        cp = pltpu.make_async_copy(out_v.at[c], out_hbm.at[:, pl.ds(c * width, width)], out_sem.at[c])
        cp.start()
        outs.append(cp)
    for cp in started:
        cp.wait_send()
    for c in range(n_chunk):
        d2d(c).wait_send()
        for k in range(1, chips):
            ici(c, k).wait_send()
        outs[c].wait()


def solution(mesh):
    pool = POOL

    def local_moe(x_loc, idx_loc, gate_loc, up_loc, down_loc):
        tok, d_model = x_loc.shape
        top_k = idx_loc.shape[1]
        n_loc, _, d_ff = up_loc.shape
        n_all = n_loc * mesh.shape['expert']
        cap = min(4, n_all // top_k) * tok * top_k // n_all
        chips, ranks = 2 * pool, 4 * pool
        n_exp = n_loc // pool
        slots = n_exp * cap
        width = d_ff // 2
        n_chunk = d_model // width
        n_up = d_ff // width
        up4 = up_loc.reshape(n_loc, 2, d_model // 2, d_ff)
        dma, f32, bf16 = pltpu.SemaphoreType.DMA, jnp.float32, jnp.bfloat16
        hbm = pl.BlockSpec(memory_space=pltpu.HBM)
        return pl.pallas_call(
            functools.partial(kernel, pool, cap),
            out_shape=jax.ShapeDtypeStruct((tok, d_model), bf16),
            in_specs=[hbm] * 5,
            out_specs=hbm,
            scratch_shapes=[
                pltpu.VMEM((RING, 2, d_ff, width), bf16),
                pltpu.VMEM((ranks, tok, d_model), bf16),
                pltpu.VMEM((ranks, top_k, tok), jnp.int32),
                pltpu.VMEM((ranks, top_k, tok), f32),
                pltpu.VMEM((ranks, slots, tok), bf16),
                pltpu.VMEM((ranks, 3 * tok, slots), bf16),
                pltpu.VMEM((n_exp, ranks * cap, d_model), bf16),
                pltpu.VMEM((n_exp, n_up, ranks * cap, width), bf16),
                pltpu.VMEM((n_exp, ranks * cap, width), bf16),
                pltpu.VMEM((n_chunk, 2, chips, tok, width), f32),
                pltpu.VMEM((n_chunk, chips, tok, width), f32),
                pltpu.VMEM((n_chunk, chips, tok, width), f32),
                pltpu.VMEM((n_chunk, chips - 1, tok, width), f32),
                pltpu.VMEM((n_chunk, tok, width), bf16),
                dma((RING,)), dma((3,)),
                dma((3, ranks - 1)), dma((3, ranks)),
                dma((n_chunk,)), dma((n_chunk,)),
                dma((n_chunk, chips - 1)), dma((n_chunk, chips - 1)),
                dma((n_chunk,)),
            ],
            compiler_params=pltpu.CompilerParams(
                collective_id=0, has_side_effects=True, vmem_limit_bytes=67043328),
            name="moe",
        )(x_loc, idx_loc.T, gate_loc.T, up4, down_loc)

    tok_spec = P(('data', 'expert'), None)
    w_spec = P('expert', None, None)
    return jax.shard_map(local_moe, mesh=mesh, in_specs=(tok_spec, tok_spec, tok_spec, w_spec, w_spec), out_specs=tok_spec, check_vma=False)
```

time: 64.6 us -> 42.2 us (0.65)
  Pallas kernels: 60.1 us -> 40.5 us
  local copies, waits for them, and re-layouts: 4.29 us -> 1.57 us
    pallas_call x1, Pallas kernels: 60.1 us -> 40.5 us  [local_moe(): pl.pallas_call(functools.partial(kernel, pool, cap), out_shape=jax.ShapeD...]
    unnamed x3 -> x1, local copies, waits for them, and re-layouts: 4.29 us -> 1.57 us
where the time goes in v2:
time: 42.2 us; the launch traced here: 42.1 us
  Pallas kernels  40.5 us (96%)
  local copies, waits for them, and re-layouts  1.57 us (4%)
    pallas_call x1, Pallas kernels, local_moe(): pl.pallas_call(functools.partial(kernel, pool, cap), out_shape=jax.ShapeD...  40.5 us
    unnamed x1, local copies, waits for them, and re-layouts  1.57 us

profile of v2, /device:TPU:0, one launch (start us, length us, event | category | flops | bytes accessed | tf_op | source)
XLA Modules:
  0.0 42.1 jit_solution(4662170345590789963)
XLA Ops:
  0.0 40.5 %moe.1 = bf16[32,2048]{1,0:T(8,128)(2,1)} custom-call(bf16[32,2048]{1,0:T(8,128)(2,1)} %x_hbm.1, s32[8,32]{1,0:T(8,128)} %bitcast.3, f32[8,32]{1,0:T(8,128)} %bitcast.4, bf16[16,2,1024,1024]{3,2,1,0:T(8,128)(2,1)} %bitcast.2.up_hbm, bf16[16,1024,2048]{2,1,0:T(8,128)(2,1)} %down_hbm.1), custom_call_target="tpu_custom_call" | custom-call | tf_op jit(solution)/shard_map/moe/pallas_call | solution.py:251
  40.5 1.6 %copy.7 = bf16[32,2048]{1,0:T(8,128)(2,1)} copy(bf16[32,2048]{1,0:T(8,128)(2,1)} %moe.1) | data formatting | bytes 262144

commit v3 on v2

v3 whole, which is shorter than its diff:
```python
import functools

import jax
import jax.numpy as jnp
from jax import lax
from jax.experimental import pallas as pl
from jax.experimental.pallas import tpu as pltpu
from jax.sharding import PartitionSpec as P

MESH = pl.DeviceIdType.MESH
POOL = 2
RING = 20
SUB = 256
GELU_C = 0.7978845608028654


def gelu(v):
    return v * (0.5 + 0.5 * jnp.tanh(v * (GELU_C + (GELU_C * 0.044715) * (v * v))))


def kernel(pool, cap, x_hbm, idx_hbm, gate_hbm, up_hbm, down_hbm, out_hbm,
           ring, xall, idx_all, gate_all, pmat, cmat, xg, part, hbuf, obuf, pacc, d2d_in, ssum, ici_in, out_v,
           ring_sem, load_sem, msend, mrecv, d2d_send, d2d_recv, ici_send, ici_recv, out_sem):
    data, expert = lax.axis_index("data"), lax.axis_index("expert")
    core = expert % 2
    y = data % pool
    chips = 2 * pool
    ranks = 2 * chips
    tok = x_hbm.shape[0]
    top_k = idx_hbm.shape[0]
    n_loc = up_hbm.shape[0]
    n_exp = n_loc // pool
    half, width = ring.shape[2:]
    n_up = up_hbm.shape[3] // width
    n_wide = down_hbm.shape[2] // width
    n_chunk = down_hbm.shape[2] // SUB
    n_pair = n_exp // 2
    half_items = n_pair * n_up
    up_items = 2 * half_items
    items = up_items + n_wide * n_pair
    first = y * n_exp
    slots = n_exp * cap

    partner = (data, expert + 1 - 2 * core)

    def chip_dev(k):
        ex = expert if k % 2 == 0 else lax.rem(expert + 2, 4)
        da = data if k < 2 else data + 1 - 2 * y
        return (da, ex)

    def weight(i):
        if i < up_items:
            k, p, n = i // half_items, i % half_items // n_up, i % n_up
            src = up_hbm.at[pl.ds(first + 2 * p, 2), k, :, pl.ds(n * width, width)]
        else:
            c, p = (i - up_items) // n_pair, (i - up_items) % n_pair
            src = down_hbm.at[pl.ds(first + 2 * p, 2), :, pl.ds(c * width, width)]
        return pltpu.make_async_copy(src, ring.at[i % RING], ring_sem.at[i % RING])

    def buf(kind, r):
        return (idx_all, gate_all)[kind].at[r] if kind < 2 else xall.at[kind - 2, r]

    loads = [pltpu.make_async_copy(src, buf(k, 0), load_sem.at[k])
             for k, src in enumerate((idx_hbm, gate_hbm, x_hbm.at[:, :half], x_hbm.at[:, half:]))]
    for cp in loads:
        cp.start()
    for i in range(min(RING, items)):
        weight(i).start(priority=1)

    barrier = pltpu.get_barrier_semaphore()
    for dev in [partner] + [chip_dev(k) for k in range(1, chips)]:
        pl.semaphore_signal(barrier, inc=1, device_id=dev, device_id_type=MESH)
    pl.semaphore_wait(barrier, chips)

    started = []

    def remote(kind, src, dst, dev):
        return pltpu.make_async_remote_copy(
            src_ref=buf(kind, src), dst_ref=buf(kind, dst),
            send_sem=msend.at[kind, dst - 1], recv_sem=mrecv.at[kind, dst],
            device_id=dev, device_id_type=MESH)

    def send(kind, src, dst, dev):
        cp = remote(kind, src, dst, dev)
        cp.start()
        started.append(cp)

    def arrived(kind, r):
        remote(kind, r, r, partner).wait_recv()

    def relay(kind, k):
        arrived(kind, 2 * k)
        send(kind, 2 * k, 2 * k + 1, partner)

    far_first = list(range(chips - 1, 0, -1))
    for kind in range(4):
        loads[kind].wait()
        for k in far_first:
            send(kind, 0, 2 * k, chip_dev(k))
        send(kind, 0, 1, partner)
    for kind in range(2):
        for k in range(1, chips):
            relay(kind, k)
    for kind in range(2):
        for k in range(chips):
            arrived(kind, 2 * k + 1)

    row = lax.broadcasted_iota(jnp.int32, (slots, tok), 0)
    eid = row // cap + (expert * n_loc + first)
    pos = (row % cap).astype(jnp.float32)
    before = (lax.broadcasted_iota(jnp.int32, (tok, tok), 0)
              < lax.broadcasted_iota(jnp.int32, (tok, tok), 1)).astype(jnp.bfloat16)
    for r in range(ranks):
        chose = jnp.zeros((slots, tok), jnp.float32)
        gate = jnp.zeros((slots, tok), jnp.float32)
        for j in range(top_k):
            hit = idx_all[r, j:j + 1, :] == eid
            chose = jnp.where(hit, 1.0, chose)
            gate = jnp.where(hit, gate_all[r, j:j + 1, :], gate)
        seen = jnp.dot(chose.astype(jnp.bfloat16), before, preferred_element_type=jnp.float32)
        one = jnp.logical_and(chose > 0.0, seen == pos)
        pmat[r] = jnp.where(one, 1.0, 0.0).astype(jnp.bfloat16)
        comb = jnp.where(one, gate, 0.0).T
        hi = comb.astype(jnp.bfloat16)
        rest = comb - hi.astype(jnp.float32)
        mid = rest.astype(jnp.bfloat16)
        low = (rest - mid.astype(jnp.float32)).astype(jnp.bfloat16)
        cmat[r, 0:tok] = hi
        cmat[r, tok:2 * tok] = mid
        cmat[r, 2 * tok:] = low

    def gather(k, r):
        for s in range(half // SUB):
            cols = slice(s * SUB, (s + 1) * SUB)
            rows = jnp.dot(pmat[r], xall[k, r, :, cols], preferred_element_type=jnp.float32)
            xg[k, :, r * cap:(r + 1) * cap, cols] = rows.astype(jnp.bfloat16).reshape(n_exp, cap, SUB)

    def up_dot(k, p, b, n, cols):
        slot = k * half_items + p * n_up + n
        return jnp.dot(xg[k, 2 * p + b], ring[slot, b, :, cols], preferred_element_type=jnp.float32)

    def up_first(p, carry):
        for b in range(2):
            for n in range(n_up):
                for s in range(width // SUB):
                    cols = slice(s * SUB, (s + 1) * SUB)
                    part[2 * p + b, n, :, cols] = up_dot(0, p, b, n, cols)
        return carry

    def up_second(p, carry):
        for b in range(2):
            for n in range(n_up):
                for s in range(width // SUB):
                    cols = slice(s * SUB, (s + 1) * SUB)
                    acc = part[2 * p + b, n, :, cols] + up_dot(1, p, b, n, cols)
                    hbuf[2 * p + b, n, :, cols] = gelu(acc).astype(jnp.bfloat16)
        return carry

    gather(0, 0)
    arrived(2, 1)
    gather(0, 1)
    for k in range(1, chips):
        relay(2, k)
        gather(0, 2 * k)
    for k in range(1, chips):
        arrived(2, 2 * k + 1)
        gather(0, 2 * k + 1)
    for i in range(half_items):
        weight(i).wait()
    lax.fori_loop(0, n_pair // 2, up_first, 0)
    for k in range(1, chips - 1):
        relay(3, k)
    lax.fori_loop(n_pair // 2, n_pair, up_first, 0)
    for i in range(RING, min(RING + half_items, items)):
        weight(i).start(priority=1)
    relay(3, chips - 1)
    gather(1, 0)
    arrived(3, 1)
    gather(1, 1)
    for k in range(1, chips):
        gather(1, 2 * k)
    for k in range(1, chips):
        arrived(3, 2 * k + 1)
        gather(1, 2 * k + 1)
    for i in range(half_items, up_items):
        weight(i).wait()
    lax.fori_loop(0, n_pair, up_second, 0)
    for i in range(RING + half_items, min(RING + up_items, items)):
        weight(i).start(priority=1)

    def d2d(c):
        return pltpu.make_async_remote_copy(
            src_ref=pacc.at[c, 1], dst_ref=d2d_in.at[c],
            send_sem=d2d_send.at[c], recv_sem=d2d_recv.at[c], device_id=partner, device_id_type=MESH)

    def ici(c, k):
        return pltpu.make_async_remote_copy(
            src_ref=ssum.at[c, k], dst_ref=ici_in.at[c, k - 1],
            send_sem=ici_send.at[c, k - 1], recv_sem=ici_recv.at[c, k - 1],
            device_id=chip_dev(k), device_id_type=MESH)

    def forward(c):
        d2d(c).wait_recv()
        ssum[c] = pacc[c, 0] + d2d_in[c]
        for k in far_first:
            ici(c, k).start()

    for c in range(n_chunk):
        wide, s = c * SUB // width, c * SUB % width
        cols = slice(s, s + SUB)
        base = up_items + wide * n_pair
        if s == 0:
            for p in range(n_pair):
                weight(base + p).wait()
        for e in range(n_exp):
            slot = (base + e // 2) % RING
            o = jnp.dot(hbuf[e, 0], ring[slot, e % 2, :width, cols], preferred_element_type=jnp.float32)
            for n in range(1, n_up):
                o += jnp.dot(hbuf[e, n], ring[slot, e % 2, n * width:(n + 1) * width, cols],
                             preferred_element_type=jnp.float32)
            obuf[e] = o.astype(jnp.bfloat16)
        for r in range(ranks):
            o = obuf[:, r * cap:(r + 1) * cap, :].reshape(slots, SUB)
            t = jnp.dot(cmat[r], o, preferred_element_type=jnp.float32)
            pacc[c, r % 2, r // 2] = t[:tok] + t[tok:2 * tok] + t[2 * tok:]
        d2d(c).start()
        if c > 0:
            forward(c - 1)
    forward(n_chunk - 1)

    outs = []
    for c in range(n_chunk):
        total = ssum[c, 0]
        for k in range(1, chips):
            ici(c, k).wait_recv()
            total += ici_in[c, k - 1]
        out_v[c] = total.astype(jnp.bfloat16)
        cp = pltpu.make_async_copy(out_v.at[c], out_hbm.at[:, pl.ds(c * SUB, SUB)], out_sem.at[c])
        cp.start()
        outs.append(cp)
    for cp in started:
        cp.wait_send()
    for c in range(n_chunk):
        d2d(c).wait_send()
        for k in range(1, chips):
            ici(c, k).wait_send()
        outs[c].wait()


def solution(mesh):
    pool = POOL

    def local_moe(x_loc, idx_loc, gate_loc, up_loc, down_loc):
        tok, d_model = x_loc.shape
        top_k = idx_loc.shape[1]
        n_loc, _, d_ff = up_loc.shape
        n_all = n_loc * mesh.shape['expert']
        cap = min(4, n_all // top_k) * tok * top_k // n_all
        chips, ranks = 2 * pool, 4 * pool
        n_exp = n_loc // pool
        slots = n_exp * cap
        width = d_ff // 2
        n_chunk = d_model // SUB
        n_up = d_ff // width
        up4 = up_loc.reshape(n_loc, 2, d_model // 2, d_ff)
        dma, f32, bf16 = pltpu.SemaphoreType.DMA, jnp.float32, jnp.bfloat16
        hbm = pl.BlockSpec(memory_space=pltpu.HBM)
        return pl.pallas_call(
            functools.partial(kernel, pool, cap),
            out_shape=jax.ShapeDtypeStruct((tok, d_model), bf16),
            in_specs=[hbm] * 5,
            out_specs=hbm,
            scratch_shapes=[
                pltpu.VMEM((RING, 2, d_ff, width), bf16),
                pltpu.VMEM((2, ranks, tok, d_model // 2), bf16),
                pltpu.VMEM((ranks, top_k, tok), jnp.int32),
                pltpu.VMEM((ranks, top_k, tok), f32),
                pltpu.VMEM((ranks, slots, tok), bf16),
                pltpu.VMEM((ranks, 3 * tok, slots), bf16),
                pltpu.VMEM((2, n_exp, ranks * cap, d_model // 2), bf16),
                pltpu.VMEM((n_exp, n_up, ranks * cap, width), f32),
                pltpu.VMEM((n_exp, n_up, ranks * cap, width), bf16),
                pltpu.VMEM((n_exp, ranks * cap, SUB), bf16),
                pltpu.VMEM((n_chunk, 2, chips, tok, SUB), f32),
                pltpu.VMEM((n_chunk, chips, tok, SUB), f32),
                pltpu.VMEM((n_chunk, chips, tok, SUB), f32),
                pltpu.VMEM((n_chunk, chips - 1, tok, SUB), f32),
                pltpu.VMEM((n_chunk, tok, SUB), bf16),
                dma((RING,)), dma((4,)),
                dma((4, ranks - 1)), dma((4, ranks)),
                dma((n_chunk,)), dma((n_chunk,)),
                dma((n_chunk, chips - 1)), dma((n_chunk, chips - 1)),
                dma((n_chunk,)),
            ],
            compiler_params=pltpu.CompilerParams(
                collective_id=0, has_side_effects=True, vmem_limit_bytes=67043328),
            name="moe",
        )(x_loc, idx_loc.T, gate_loc.T, up4, down_loc)

    tok_spec = P(('data', 'expert'), None)
    w_spec = P('expert', None, None)
    return jax.shard_map(local_moe, mesh=mesh, in_specs=(tok_spec, tok_spec, tok_spec, w_spec, w_spec), out_specs=tok_spec, check_vma=False)
```

time: 42.2 us -> 38.5 us (0.912)
  Pallas kernels: 40.5 us -> 36.9 us
    pallas_call x1, Pallas kernels: 40.5 us -> 36.9 us  [local_moe(): pl.pallas_call(functools.partial(kernel, pool, cap), out_shape=jax.ShapeD...]
where the time goes in v3:
time: 38.5 us; the launch traced here: 38.4 us
  Pallas kernels  36.9 us (96%)
  local copies, waits for them, and re-layouts  1.57 us (4%)
    pallas_call x1, Pallas kernels, local_moe(): pl.pallas_call(functools.partial(kernel, pool, cap), out_shape=jax.ShapeD...  36.9 us
    unnamed x1, local copies, waits for them, and re-layouts  1.57 us

profile of v3, /device:TPU:0, one launch (start us, length us, event | category | flops | bytes accessed | tf_op | source)
XLA Modules:
  0.0 38.4 jit_solution(2638536431918942277)
XLA Ops:
  0.0 36.9 %moe.1 = bf16[32,2048]{1,0:T(8,128)(2,1)} custom-call(bf16[32,2048]{1,0:T(8,128)(2,1)} %x_hbm.1, s32[8,32]{1,0:T(8,128)} %bitcast.3, f32[8,32]{1,0:T(8,128)} %bitcast.4, bf16[16,2,1024,1024]{3,2,1,0:T(8,128)(2,1)} %bitcast.2.up_hbm, bf16[16,1024,2048]{2,1,0:T(8,128)(2,1)} %down_hbm.1), custom_call_target="tpu_custom_call" | custom-call | tf_op jit(solution)/shard_map/moe/pallas_call | solution.py:268
  36.9 1.6 %copy.7 = bf16[32,2048]{1,0:T(8,128)(2,1)} copy(bf16[32,2048]{1,0:T(8,128)(2,1)} %moe.1) | data formatting | bytes 262144

commit v4 on v3

--- a/solution.py
+++ b/solution.py
@@ -11,6 +11,8 @@
 POOL = 2
 RING = 20
 SUB = 256
+STAGED = 7
+LAG = 4
 GELU_C = 0.7978845608028654
 
 
@@ -159,6 +161,9 @@
     gather(0, 0)
     arrived(2, 1)
     gather(0, 1)
+    gather(1, 0)
+    arrived(3, 1)
+    gather(1, 1)
     for k in range(1, chips):
         relay(2, k)
         gather(0, 2 * k)
@@ -167,16 +172,12 @@
         gather(0, 2 * k + 1)
     for i in range(half_items):
         weight(i).wait()
-    lax.fori_loop(0, n_pair // 2, up_first, 0)
-    for k in range(1, chips - 1):
+    lax.fori_loop(0, n_pair // 2, up_first, 0, unroll=True)
+    for k in range(1, chips):
         relay(3, k)
-    lax.fori_loop(n_pair // 2, n_pair, up_first, 0)
+    lax.fori_loop(n_pair // 2, n_pair, up_first, 0, unroll=True)
     for i in range(RING, min(RING + half_items, items)):
         weight(i).start(priority=1)
-    relay(3, chips - 1)
-    gather(1, 0)
-    arrived(3, 1)
-    gather(1, 1)
     for k in range(1, chips):
         gather(1, 2 * k)
     for k in range(1, chips):
@@ -184,7 +185,7 @@
         gather(1, 2 * k + 1)
     for i in range(half_items, up_items):
         weight(i).wait()
-    lax.fori_loop(0, n_pair, up_second, 0)
+    lax.fori_loop(0, n_pair, up_second, 0, unroll=True)
     for i in range(RING + half_items, min(RING + up_items, items)):
         weight(i).start(priority=1)
 
@@ -193,17 +194,43 @@
             src_ref=pacc.at[c, 1], dst_ref=d2d_in.at[c],
             send_sem=d2d_send.at[c], recv_sem=d2d_recv.at[c], device_id=partner, device_id_type=MESH)
 
-    def ici(c, k):
+    lanes = SUB // 2
+    order = ((1, 2), (2, 1))
+
+    def ici(c, h, j, src, dst, k):
         return pltpu.make_async_remote_copy(
-            src_ref=ssum.at[c, k], dst_ref=ici_in.at[c, k - 1],
-            send_sem=ici_send.at[c, k - 1], recv_sem=ici_recv.at[c, k - 1],
+            src_ref=ssum.at[c, h, src], dst_ref=ici_in.at[c, h, dst],
+            send_sem=ici_send.at[c, h, j], recv_sem=ici_recv.at[c, h, j],
             device_id=chip_dev(k), device_id_type=MESH)
+
+    def hop(c, h, j):
+        a, b = order[h]
+        if c < STAGED:
+            return ici(c, h, 0, pl.ds(2, 2), pl.ds(0, 2), a) if j == 0 else ici(c, h, 1, 1, 2, b)
+        return ici(c, h, j, j + 1, j, (b, a, 3)[j])
+
+    def n_hops(c):
+        return 2 if c < STAGED else 3
 
     def forward(c):
         d2d(c).wait_recv()
-        ssum[c] = pacc[c, 0] + d2d_in[c]
-        for k in far_first:
-            ici(c, k).start()
+        for h, (a, b) in enumerate(order):
+            for slot, k in enumerate((0, b, a, 3)):
+                cols = slice(h * lanes, (h + 1) * lanes)
+                ssum[c, h, slot] = pacc[c, 0, k, :, cols] + d2d_in[c, k, :, cols]
+        if c < STAGED:
+            for h in range(2):
+                hop(c, h, 0).start()
+        else:
+            for j in range(2, -1, -1):
+                for h in range(2):
+                    hop(c, h, j).start()
+
+    def second_hop(c):
+        for h in range(2):
+            hop(c, h, 0).wait_recv()
+            ssum[c, h, 1] = ssum[c, h, 1] + ici_in[c, h, 1]
+            hop(c, h, 1).start()
 
     for c in range(n_chunk):
         wide, s = c * SUB // width, c * SUB % width
@@ -226,15 +253,23 @@
         d2d(c).start()
         if c > 0:
             forward(c - 1)
+        if 0 <= c - LAG < STAGED:
+            second_hop(c - LAG)
     forward(n_chunk - 1)
+    for c in range(n_chunk - LAG, STAGED):
+        second_hop(c)
 
     outs = []
     for c in range(n_chunk):
-        total = ssum[c, 0]
-        for k in range(1, chips):
-            ici(c, k).wait_recv()
-            total += ici_in[c, k - 1]
-        out_v[c] = total.astype(jnp.bfloat16)
+        for h in range(2):
+            if c < STAGED:
+                hop(c, h, 1).wait_recv()
+                total = ssum[c, h, 0] + ici_in[c, h, 0] + ici_in[c, h, 2]
+            else:
+                for j in range(3):
+                    hop(c, h, j).wait_recv()
+                total = ssum[c, h, 0] + ici_in[c, h, 0] + ici_in[c, h, 1] + ici_in[c, h, 2]
+            out_v[c, :, h * lanes:(h + 1) * lanes] = total.astype(jnp.bfloat16)
         cp = pltpu.make_async_copy(out_v.at[c], out_hbm.at[:, pl.ds(c * SUB, SUB)], out_sem.at[c])
         cp.start()
         outs.append(cp)
@@ -242,8 +277,9 @@
         cp.wait_send()
     for c in range(n_chunk):
         d2d(c).wait_send()
-        for k in range(1, chips):
-            ici(c, k).wait_send()
+        for h in range(2):
+            for j in range(n_hops(c)):
+                hop(c, h, j).wait_send()
         outs[c].wait()
 
 
@@ -283,13 +319,13 @@
                 pltpu.VMEM((n_exp, ranks * cap, SUB), bf16),
                 pltpu.VMEM((n_chunk, 2, chips, tok, SUB), f32),
                 pltpu.VMEM((n_chunk, chips, tok, SUB), f32),
-                pltpu.VMEM((n_chunk, chips, tok, SUB), f32),
-                pltpu.VMEM((n_chunk, chips - 1, tok, SUB), f32),
+                pltpu.VMEM((n_chunk, 2, chips, tok, SUB // 2), f32),
+                pltpu.VMEM((n_chunk, 2, chips - 1, tok, SUB // 2), f32),
                 pltpu.VMEM((n_chunk, tok, SUB), bf16),
                 dma((RING,)), dma((4,)),
                 dma((4, ranks - 1)), dma((4, ranks)),
                 dma((n_chunk,)), dma((n_chunk,)),
-                dma((n_chunk, chips - 1)), dma((n_chunk, chips - 1)),
+                dma((n_chunk, 2, chips - 1)), dma((n_chunk, 2, chips - 1)),
                 dma((n_chunk,)),
             ],
             compiler_params=pltpu.CompilerParams(

time: 38.5 us -> 36.1 us (0.938)
  Pallas kernels: 36.9 us -> 34.4 us
    pallas_call x1, Pallas kernels: 36.9 us -> 34.4 us  [local_moe(): pl.pallas_call(functools.partial(kernel, pool, cap), out_shape=jax.ShapeD...]
where the time goes in v4:
time: 36.1 us; the launch traced here: 36 us
  Pallas kernels  34.4 us (95%)
  local copies, waits for them, and re-layouts  1.57 us (4%)
    pallas_call x1, Pallas kernels, local_moe(): pl.pallas_call(functools.partial(kernel, pool, cap), out_shape=jax.ShapeD...  34.4 us
    unnamed x1, local copies, waits for them, and re-layouts  1.57 us

profile of v4, /device:TPU:0, one launch (start us, length us, event | category | flops | bytes accessed | tf_op | source)
XLA Modules:
  0.0 36.0 jit_solution(15932612234539652793)
XLA Ops:
  0.0 34.4 %moe.1 = bf16[32,2048]{1,0:T(8,128)(2,1)} custom-call(bf16[32,2048]{1,0:T(8,128)(2,1)} %x_hbm.1, s32[8,32]{1,0:T(8,128)} %bitcast.3, f32[8,32]{1,0:T(8,128)} %bitcast.4, bf16[16,2,1024,1024]{3,2,1,0:T(8,128)(2,1)} %bitcast.2.up_hbm, bf16[16,1024,2048]{2,1,0:T(8,128)(2,1)} %down_hbm.1), custom_call_target="tpu_custom_call" | custom-call | tf_op jit(solution)/shard_map/moe/pallas_call | solution.py:304
  34.4 1.6 %copy.7 = bf16[32,2048]{1,0:T(8,128)(2,1)} copy(bf16[32,2048]{1,0:T(8,128)(2,1)} %moe.1) | data formatting | bytes 262144

commit v5 on v4

--- a/solution.py
+++ b/solution.py
@@ -46,7 +46,7 @@
     partner = (data, expert + 1 - 2 * core)
 
     def chip_dev(k):
-        ex = expert if k % 2 == 0 else lax.rem(expert + 2, 4)
+        ex = partner[1] if k % 2 == 0 else lax.rem(partner[1] + 2, 4)
         da = data if k < 2 else data + 1 - 2 * y
         return (da, ex)
 
@@ -91,38 +91,46 @@
         remote(kind, r, r, partner).wait_recv()
 
     def relay(kind, k):
-        arrived(kind, 2 * k)
-        send(kind, 2 * k, 2 * k + 1, partner)
+        arrived(kind, 2 * k + 1)
+        send(kind, 2 * k + 1, 2 * k, partner)
 
     far_first = list(range(chips - 1, 0, -1))
     for kind in range(4):
         loads[kind].wait()
         for k in far_first:
-            send(kind, 0, 2 * k, chip_dev(k))
+            send(kind, 0, 2 * k + 1, chip_dev(k))
         send(kind, 0, 1, partner)
     for kind in range(2):
         for k in range(1, chips):
             relay(kind, k)
     for kind in range(2):
-        for k in range(chips):
-            arrived(kind, 2 * k + 1)
-
-    row = lax.broadcasted_iota(jnp.int32, (slots, tok), 0)
-    eid = row // cap + (expert * n_loc + first)
-    pos = (row % cap).astype(jnp.float32)
+        arrived(kind, 1)
+        for k in range(1, chips):
+            arrived(kind, 2 * k)
+
+    eid = lax.broadcasted_iota(jnp.int32, (n_exp, tok), 0) + (expert * n_loc + first)
+    pos = (lax.broadcasted_iota(jnp.int32, (slots, tok), 0) % cap).astype(jnp.float32)
     before = (lax.broadcasted_iota(jnp.int32, (tok, tok), 0)
               < lax.broadcasted_iota(jnp.int32, (tok, tok), 1)).astype(jnp.bfloat16)
+    gates = []
     for r in range(ranks):
-        chose = jnp.zeros((slots, tok), jnp.float32)
-        gate = jnp.zeros((slots, tok), jnp.float32)
+        gate = jnp.full((n_exp, tok), -1.0)
         for j in range(top_k):
-            hit = idx_all[r, j:j + 1, :] == eid
-            chose = jnp.where(hit, 1.0, chose)
-            gate = jnp.where(hit, gate_all[r, j:j + 1, :], gate)
-        seen = jnp.dot(chose.astype(jnp.bfloat16), before, preferred_element_type=jnp.float32)
-        one = jnp.logical_and(chose > 0.0, seen == pos)
+            gate = jnp.where(idx_all[r, j:j + 1, :] == eid, gate_all[r, j:j + 1, :], gate)
+        gates.append(gate)
+    gates = jnp.concatenate(gates, axis=0)
+    chose = jnp.where(gates >= 0.0, 1.0, 0.0)
+    seen = jnp.dot(chose.astype(jnp.bfloat16), before, preferred_element_type=jnp.float32)
+    place = jnp.where(gates >= 0.0, seen, -1.0)
+
+    def spread(a, r):
+        a = a[r * n_exp:(r + 1) * n_exp]
+        return jnp.broadcast_to(a[:, None, :], (n_exp, cap, tok)).reshape(slots, tok)
+
+    for r in range(ranks):
+        one = spread(place, r) == pos
         pmat[r] = jnp.where(one, 1.0, 0.0).astype(jnp.bfloat16)
-        comb = jnp.where(one, gate, 0.0).T
+        comb = jnp.where(one, spread(gates, r), 0.0).T
         hi = comb.astype(jnp.bfloat16)
         rest = comb - hi.astype(jnp.float32)
         mid = rest.astype(jnp.bfloat16)
@@ -162,27 +170,29 @@
     arrived(2, 1)
     gather(0, 1)
     gather(1, 0)
+    for k in range(1, chips):
+        relay(2, k)
+    for k in range(1, chips):
+        gather(0, 2 * k + 1)
     arrived(3, 1)
     gather(1, 1)
     for k in range(1, chips):
-        relay(2, k)
+        arrived(2, 2 * k)
+    for k in range(1, chips):
         gather(0, 2 * k)
-    for k in range(1, chips):
-        arrived(2, 2 * k + 1)
-        gather(0, 2 * k + 1)
     for i in range(half_items):
         weight(i).wait()
-    lax.fori_loop(0, n_pair // 2, up_first, 0, unroll=True)
+    lax.fori_loop(0, n_pair - 1, up_first, 0, unroll=True)
     for k in range(1, chips):
         relay(3, k)
-    lax.fori_loop(n_pair // 2, n_pair, up_first, 0, unroll=True)
+    lax.fori_loop(n_pair - 1, n_pair, up_first, 0, unroll=True)
     for i in range(RING, min(RING + half_items, items)):
         weight(i).start(priority=1)
     for k in range(1, chips):
+        arrived(3, 2 * k)
+    for k in range(1, chips):
+        gather(1, 2 * k + 1)
         gather(1, 2 * k)
-    for k in range(1, chips):
-        arrived(3, 2 * k + 1)
-        gather(1, 2 * k + 1)
     for i in range(half_items, up_items):
         weight(i).wait()
     lax.fori_loop(0, n_pair, up_second, 0, unroll=True)
@@ -231,6 +241,10 @@
             hop(c, h, 0).wait_recv()
             ssum[c, h, 1] = ssum[c, h, 1] + ici_in[c, h, 1]
             hop(c, h, 1).start()
+
+    def side(c, r):
+        crossings = (0, 1, 1, 2 if c < STAGED else 1)[r // 2]
+        return (r + crossings) % 2
 
     for c in range(n_chunk):
         wide, s = c * SUB // width, c * SUB % width
@@ -249,7 +263,7 @@
         for r in range(ranks):
             o = obuf[:, r * cap:(r + 1) * cap, :].reshape(slots, SUB)
             t = jnp.dot(cmat[r], o, preferred_element_type=jnp.float32)
-            pacc[c, r % 2, r // 2] = t[:tok] + t[tok:2 * tok] + t[2 * tok:]
+            pacc[c, side(c, r), r // 2] = t[:tok] + t[tok:2 * tok] + t[2 * tok:]
         d2d(c).start()
         if c > 0:
             forward(c - 1)

time: 36.1 us -> 35.4 us (0.981)
  Pallas kernels: 34.4 us -> 33.7 us
    pallas_call x1, Pallas kernels: 34.4 us -> 33.7 us  [local_moe(): pl.pallas_call(functools.partial(kernel, pool, cap), out_shape=jax.ShapeD...]
where the time goes in v5:
time: 35.4 us; the launch traced here: 35.2 us
  Pallas kernels  33.7 us (95%)
  local copies, waits for them, and re-layouts  1.57 us (4%)
    pallas_call x1, Pallas kernels, local_moe(): pl.pallas_call(functools.partial(kernel, pool, cap), out_shape=jax.ShapeD...  33.7 us
    unnamed x1, local copies, waits for them, and re-layouts  1.57 us

profile of v5, /device:TPU:0, one launch (start us, length us, event | category | flops | bytes accessed | tf_op | source)
XLA Modules:
  0.0 35.2 jit_solution(4358278690371639553)
XLA Ops:
  0.0 33.7 %moe.1 = bf16[32,2048]{1,0:T(8,128)(2,1)} custom-call(bf16[32,2048]{1,0:T(8,128)(2,1)} %x_hbm.1, s32[8,32]{1,0:T(8,128)} %bitcast.3, f32[8,32]{1,0:T(8,128)} %bitcast.4, bf16[16,2,1024,1024]{3,2,1,0:T(8,128)(2,1)} %bitcast.2.up_hbm, bf16[16,1024,2048]{2,1,0:T(8,128)(2,1)} %down_hbm.1), custom_call_target="tpu_custom_call" | custom-call | tf_op jit(solution)/shard_map/moe/pallas_call | solution.py:318
  33.7 1.6 %copy.7 = bf16[32,2048]{1,0:T(8,128)(2,1)} copy(bf16[32,2048]{1,0:T(8,128)(2,1)} %moe.1) | data formatting | bytes 262144

commit v6 on v5

--- a/solution.py
+++ b/solution.py
@@ -182,10 +182,10 @@
         gather(0, 2 * k)
     for i in range(half_items):
         weight(i).wait()
-    lax.fori_loop(0, n_pair - 1, up_first, 0, unroll=True)
+    lax.fori_loop(0, n_pair // 2, up_first, 0, unroll=True)
     for k in range(1, chips):
         relay(3, k)
-    lax.fori_loop(n_pair - 1, n_pair, up_first, 0, unroll=True)
+    lax.fori_loop(n_pair // 2, n_pair, up_first, 0, unroll=True)
     for i in range(RING, min(RING + half_items, items)):
         weight(i).start(priority=1)
     for k in range(1, chips):
@@ -217,14 +217,18 @@
         a, b = order[h]
         if c < STAGED:
             return ici(c, h, 0, pl.ds(2, 2), pl.ds(0, 2), a) if j == 0 else ici(c, h, 1, 1, 2, b)
-        return ici(c, h, j, j + 1, j, (b, a, 3)[j])
+        return pltpu.make_async_remote_copy(
+            src_ref=ssum.at[c, :, j + 1], dst_ref=ici_in.at[c, :, j],
+            send_sem=ici_send.at[c, 0, j], recv_sem=ici_recv.at[c, 0, j],
+            device_id=chip_dev((2, 1, 3)[j]), device_id_type=MESH)
 
     def n_hops(c):
         return 2 if c < STAGED else 3
 
     def forward(c):
         d2d(c).wait_recv()
-        for h, (a, b) in enumerate(order):
+        for h in range(2):
+            a, b = order[h if c < STAGED else 0]
             for slot, k in enumerate((0, b, a, 3)):
                 cols = slice(h * lanes, (h + 1) * lanes)
                 ssum[c, h, slot] = pacc[c, 0, k, :, cols] + d2d_in[c, k, :, cols]
@@ -233,8 +237,7 @@
                 hop(c, h, 0).start()
         else:
             for j in range(2, -1, -1):
-                for h in range(2):
-                    hop(c, h, j).start()
+                hop(c, 0, j).start()
 
     def second_hop(c):
         for h in range(2):
@@ -280,8 +283,9 @@
                 hop(c, h, 1).wait_recv()
                 total = ssum[c, h, 0] + ici_in[c, h, 0] + ici_in[c, h, 2]
             else:
-                for j in range(3):
-                    hop(c, h, j).wait_recv()
+                if h == 0:
+                    for j in range(3):
+                        hop(c, 0, j).wait_recv()
                 total = ssum[c, h, 0] + ici_in[c, h, 0] + ici_in[c, h, 1] + ici_in[c, h, 2]
             out_v[c, :, h * lanes:(h + 1) * lanes] = total.astype(jnp.bfloat16)
         cp = pltpu.make_async_copy(out_v.at[c], out_hbm.at[:, pl.ds(c * SUB, SUB)], out_sem.at[c])
@@ -291,7 +295,7 @@
         cp.wait_send()
     for c in range(n_chunk):
         d2d(c).wait_send()
-        for h in range(2):
+        for h in range(2 if c < STAGED else 1):
             for j in range(n_hops(c)):
                 hop(c, h, j).wait_send()
         outs[c].wait()

time: 35.4 us -> 35.3 us (level)
  no operation moved by 1% of the time
where the time goes in v6:
time: 35.3 us; the launch traced here: 35.2 us
  Pallas kernels  33.6 us (95%)
  local copies, waits for them, and re-layouts  1.57 us (4%)
    pallas_call x1, Pallas kernels, local_moe(): pl.pallas_call(functools.partial(kernel, pool, cap), out_shape=jax.ShapeD...  33.6 us
    unnamed x1, local copies, waits for them, and re-layouts  1.57 us

profile of v6, /device:TPU:0, one launch (start us, length us, event | category | flops | bytes accessed | tf_op | source)
XLA Modules:
  0.0 35.2 jit_solution(13038571028002552943)
XLA Ops:
  0.0 33.6 %moe.1 = bf16[32,2048]{1,0:T(8,128)(2,1)} custom-call(bf16[32,2048]{1,0:T(8,128)(2,1)} %x_hbm.1, s32[8,32]{1,0:T(8,128)} %bitcast.3, f32[8,32]{1,0:T(8,128)} %bitcast.4, bf16[16,2,1024,1024]{3,2,1,0:T(8,128)(2,1)} %bitcast.2.up_hbm, bf16[16,1024,2048]{2,1,0:T(8,128)(2,1)} %down_hbm.1), custom_call_target="tpu_custom_call" | custom-call | tf_op jit(solution)/shard_map/moe/pallas_call | solution.py:322
  33.6 1.6 %copy.7 = bf16[32,2048]{1,0:T(8,128)(2,1)} copy(bf16[32,2048]{1,0:T(8,128)(2,1)} %moe.1) | data formatting | bytes 262144
